TPU v7x, 32 devices: a whole 2x2x4 slice. The times are simulated.
32 devices in a mesh: grp: 4 (over y, x), seq: 8 (over z, core).
Axes of the slice: x: 2, y: 2, z: 4, core: 2. Of those that a mesh axis runs over, the one named last changes fastest.
Arguments:
- queries: bfloat16 [8192, 2048], P(('grp', 'seq')), may hold values from -48 to 48
- key_rows: bfloat16 [8192, 512], P(('grp', 'seq')), may hold values from -4.5 to 4.5
- value_rows: bfloat16 [8192, 512], P(('grp', 'seq')), may hold values from -6 to 6
- segments: int32 [8192], P(('grp', 'seq')), may hold values from 0 to 3, as said below
Outputs:
- attended: bfloat16 [8192, 2048], P(('grp', 'seq'))
- log_sums: float32 [16, 8192], P(None, ('grp', 'seq'))
Inputs may be any that keep to these rules, and one draw needn't show every extreme that they name: `segments`: never falls along the sequence, starts at 0 and rises by one at each new document; the last token holds the largest value.
All inputs are finite; a program needn't handle non-finite values.
Results may differ from a plain program's by a relative error of at most 0.0035.
Values may be sent and summed in bfloat16 or wider, within the bound.
A program may use at most 192 MiB of HBM per device.

v0:
```python
import functools
import heapq
import math

import jax
import jax.numpy as jnp
from jax import lax
from jax.experimental import pallas as pl
from jax.experimental.pallas import tpu as pltpu
from jax.sharding import PartitionSpec as P

Q_HEADS = 16
KV_HEADS = 4
HEAD_DIM = 128
WINDOW = 4096
AXES = ("grp", "seq")
LOW = -1e30


def block_step(qt, k_ref, v_ref, m_ref, l_ref, acc, bias):
    c = math.log2(math.e) / math.sqrt(HEAD_DIM)
    group = Q_HEADS // KV_HEADS

    def scores(h):
        g = h // group
        return jnp.dot(
            k_ref[:, g * HEAD_DIM : (g + 1) * HEAD_DIM], qt[h], preferred_element_type=jnp.float32
        )

    def summed(h, p, alpha):
        g = h // group
        if h % group == 0:
            vts[g] = v_ref[:, g * HEAD_DIM : (g + 1) * HEAD_DIM].T
        acc[h] = acc[h] * alpha + jnp.dot(vts[g], p, preferred_element_type=jnp.float32)

    vts = {}
    AHEAD = 2
    ready = [scores(h) for h in range(AHEAD)]
    waiting = None
    for h in range(Q_HEADS):
        if h + AHEAD < Q_HEADS:
            ready.append(scores(h + AHEAD))
        s = ready.pop(0)
        if bias is not None:
            s = s + bias[...]
        m_old = m_ref[h]
        m_new = jnp.maximum(m_old, jnp.max(s, axis=0, keepdims=True))
        p = jnp.exp2((s - m_new) * c)
        alpha = jnp.exp2((m_old - m_new) * c)
        l_ref[h] = l_ref[h] * alpha + jnp.sum(p, axis=0, keepdims=True)
        m_ref[h] = m_new
        if waiting is not None:
            summed(*waiting)
        waiting = (h, p.astype(jnp.bfloat16), alpha)
    summed(*waiting)


def flash(info, lower_ref, q_ref, k_ref, v_ref, o_ref, ls_ref, qt, m_ref, l_ref, acc, bias):
    j = pl.program_id(0)
    tok = q_ref.shape[0]
    device, first, clean = info[0], info[1], info[2]

    @pl.when(j == 0)
    def _():
        for h in range(Q_HEADS):
            qt[h] = q_ref[:, h * HEAD_DIM : (h + 1) * HEAD_DIM].T
        m_ref[...] = jnp.full_like(m_ref, LOW)
        l_ref[...] = jnp.zeros_like(l_ref)
        acc[...] = jnp.zeros_like(acc)

    block = device - j
    edge = (j == 0) | (block < clean)

    @pl.when((block >= first) & edge)
    def _():
        key_pos = block * tok + lax.broadcasted_iota(jnp.int32, (tok, tok), 0)
        pos = device * tok + lax.broadcasted_iota(jnp.int32, (tok, tok), 1)
        allowed = (key_pos >= lower_ref[...]) & (key_pos <= pos)
        bias[...] = jnp.where(allowed, 0.0, LOW)
        block_step(qt, k_ref, v_ref, m_ref, l_ref, acc, bias)

    @pl.when((block >= first) & jnp.logical_not(edge))
    def _():
        block_step(qt, k_ref, v_ref, m_ref, l_ref, acc, None)

    @pl.when(j == pl.num_programs(0) - 1)
    def _():
        for h in range(Q_HEADS):
            out = acc[h] * (1.0 / l_ref[h])
            o_ref[:, h * HEAD_DIM : (h + 1) * HEAD_DIM] = out.T.astype(o_ref.dtype)
            ls_ref[h : h + 1, :] = m_ref[h] * (1.0 / math.sqrt(HEAD_DIM)) + jnp.log(l_ref[h])


def routes(n, c, z, g, s, j):
    other = z + 1 - 2 * (z % 2)
    cross = not (s == other and j == 1)
    near, far = s == 1 and j == 1, s == n - 1 and j == 1
    up, down = z + 1 < n and s <= z, z > 0 and s >= z
    out = []
    if c in (0, 2) and g == c:
        if up:
            out.append(0)
        if down and not (c == 2 and z == 1 and (near or far)):
            out.append(1)
        if cross and not (c == 2 and z == 0 and far):
            out.append(2)
        if c == 0 and s >= z and not (z == 0 and near):
            out.append(3)
    elif c == 0 and g == 1:
        out.append(3)
    elif c == 1 and g == 1:
        if up:
            out.append(0)
        if down:
            out.append(1)
        if s < z and j == 1:
            out.append(2)
        elif not (z == 0 and near):
            out.append(3)
    elif c in (1, 3) and g == c - 1:
        if s == z and j == 1:
            out.append(z % 2)
        elif c == 3 and z == 1 and far:
            out.append(1)
    elif c == 2:
        if g == 0 and z == 1 and near:
            out.append(1)
        if g == 1 and (z in (1, n - 2) and far or z == 1 and s == n - 1):
            out.append(1)
    elif c == 3 and g == 3:
        if up:
            out.append(0)
    elif c == 3 and g == 1:
        if not (z <= 1 and far or z == 0 and s == n - 1):
            out.append(2)
        if z == 1 and near:
            out.append(1)
    return out


def step_to(c, z, d):
    return ((c, z + 1), (c, z - 1), (c ^ 1, z), (c ^ 2, z))[d]


def needed(c, z, g, s):
    return (g == c and s <= z) or g == c - 1 or (g == c - 2 and s >= z)


LOCAL, SIBLING, LINK, SEND, COMPUTE = range(5)


def schedule(n, chunk=2.95, flight=1.7, work=1.8, ahead=2.5, ready=4.5):
    chips = [(c, z) for c in range(4) for z in range(n)]

    @functools.lru_cache(None)
    def depth(c, z, g, s, j):
        return max((1 + depth(*step_to(c, z, d), g, s, j) for d in routes(n, c, z, g, s, j)), default=0)

    free, seen, inbox, pend, have, clock, prog, todo = {}, {}, {}, {}, {}, {}, {}, {}
    order = 0
    for c, z in chips:
        ch = c, z
        own = [(2.0 + 1.5 * b, -j, (c, z, j, b)) for b in (0, 1) for j in (1, 0)]
        inbox[ch], have[ch], clock[ch], prog[ch], todo[ch] = own, [], 2.0, [], []
        seen[ch] = [u for _, _, u in own]
        for d in range(4):
            free[ch, d], pend[ch, d] = 0.0, []

    def issue(ch, d, t):
        u = heapq.heappop(pend[ch, d])[2]
        to = step_to(*ch, d)
        free[ch, d] = max(free[ch, d], t) + chunk
        assert u not in seen[to]
        seen[to].append(u)
        heapq.heappush(inbox[to], (free[ch, d] + flight, 0, u))
        return u

    def options(ch):
        t = clock[ch]
        for d in range(4):
            if pend[ch, d]:
                yield max(t, free[ch, d] - ahead), 0, ch, d
        if inbox[ch]:
            yield max(t, inbox[ch][0][0]), 1, ch, 0
        if todo[ch]:
            yield max(t, ready), 2, ch, 0

    while True:
        best = min((o for ch in chips for o in options(ch)), default=None)
        if best is None:
            break
        t, kind, ch, d = best
        if kind == 0:
            prog[ch].append((SEND, issue(ch, d, t), 1 << d))
            clock[ch] = t + 0.05
        elif kind == 1:
            u = heapq.heappop(inbox[ch])[2]
            g, s, j, b = u
            mask = 0
            for d in routes(n, *ch, g, s, j):
                order += 1
                heapq.heappush(pend[ch, d], (-depth(*step_to(*ch, d), g, s, j), order, u))
                if free[ch, d] - ahead <= t and pend[ch, d][0][2] == u:
                    issue(ch, d, t)
                    mask |= 1 << d
            op = LINK if (g, s) != ch else (LOCAL, SIBLING)[b]
            prog[ch].append((op, u, mask))
            clock[ch] = t + 0.1
            have[ch].append(u)
            if needed(*ch, g, s) and (g, s, j, 1 - b) in have[ch]:
                todo[ch].append((g, s, j, 0))
        else:
            todo[ch].sort(key=lambda u: (u[0], u[1]) != ch)
            prog[ch].append((COMPUTE, todo[ch].pop(0), 0))
            clock[ch] = max(t, ready) + work
    for ch in chips:
        done = [u[:3] for op, u, _ in prog[ch] if op == COMPUTE]
        want = [(g, s, j) for g in range(4) for s in range(n) for j in range(2) if needed(*ch, g, s)]
        assert sorted(done) == want

    def word(op, u, mask):
        g, s, j, b = u
        return op + 8 * (b + 2 * (mask + 16 * ((g * n + s) * 2 + j)))

    moves, stops, works = [], [], []
    for ch in chips:
        stop, work = [], []
        for op, u, _ in prog[ch]:
            if op == COMPUTE:
                stop.append(len([e for e in prog[ch][: prog[ch].index((op, u, 0))] if e[0] != COMPUTE]))
                work.append((u[0] * n + u[1]) * 2 + u[2])
        move = [word(*e) for e in prog[ch] if e[0] != COMPUTE]
        moves.append(move)
        stops.append(stop + [len(move)])
        works.append(work)
    steps = max(len(w) for w in works)
    counts = [len(w) for w in works]
    stops = [s[:-1] + [s[-1]] * (steps + 1 - len(s) + 1) for s in stops]
    works = [w + [w[-1]] * (steps - len(w)) for w in works]
    return moves, stops, works, counts


def pick(words, bits):
    for bit in bits:
        if len(words) == 1:
            break
        pairs = [(words[i], words[min(i + 1, len(words) - 1)]) for i in range(0, len(words), 2)]
        words = [
            lo if isinstance(lo, int) and isinstance(hi, int) and lo == hi else jnp.where(bit, jnp.int32(hi), jnp.int32(lo))
            for lo, hi in pairs
        ]
    return words[0]


def exchange_attend(n, k_in, v_in, q_in, seg_in, o_out, ls_out, table, ends, c_in, s_in, kv, qraw, segs, qt, m_ref, acc, obuf, lsbuf, seg_here,
                    local, sib_send, sib_recv, link_send, link_recv):
    tok = k_in.shape[0]
    heads = Q_HEADS // 2
    group = Q_HEADS // KV_HEADS
    scale = math.log2(math.e) / math.sqrt(HEAD_DIM)
    c, s = lax.axis_index("grp"), lax.axis_index("seq")
    z, k = lax.div(s, 2), lax.rem(s, 2)
    sib = s + 1 - 2 * k
    row, col = lax.div(c, 2), lax.rem(c, 2)
    peers = (
        (z + 1 < n, (c, s + 2)),
        (z > 0, (c, s - 2)),
        (c >= 0, (c + 1 - 2 * col, s)),
        (c >= 0, (c + 2 - 4 * row, s)),
        (c >= 0, (c, sib)),
    )
    here = (c * n + z) * 2

    def parts(core):
        made = []
        for j in range(2):
            cols = pl.ds(pl.multiple_of((2 * core + j) * HEAD_DIM, HEAD_DIM), HEAD_DIM)
            for t, src in enumerate((k_in.at[:, cols], v_in.at[:, cols], c_in)):
                rows = pl.ds(t * tok, src.shape[0])
                made.append((src, kv.at[here + j, k, rows, :], 3 * j + t))
        cols = pl.ds(pl.multiple_of(core * heads * HEAD_DIM, HEAD_DIM), heads * HEAD_DIM)
        made.append((q_in.at[:, cols], qraw.at[k], 6))
        made.append((s_in, segs.at[k], 7))
        return made

    def to_sib(src, dst, i):
        return pltpu.make_async_remote_copy(
            src_ref=src, dst_ref=dst, send_sem=sib_send.at[i], recv_sem=sib_recv.at[i],
            device_id=(c, sib), device_id_type=pl.DeviceIdType.MESH,
        )

    mine = {i: pltpu.make_async_copy(src, dst, local.at[i]) for src, dst, i in parts(k) if i in (0, 1, 3, 4, 6)}
    theirs = [to_sib(src, dst, i) for src, dst, i in parts(1 - k)]

    def coming(j, t):
        rows = pl.ds(t * tok, tok if t < 2 else c_in.shape[0])
        ref = kv.at[here + j, 1 - k, rows, :]
        return to_sib(ref, ref, 3 * j + t)

    fetch = pltpu.make_async_copy(seg_in, seg_here, local.at[7])
    fetch.start()
    for copy in mine.values():
        copy.start()
    barrier = pltpu.get_barrier_semaphore()
    count = 0
    for ok, to in peers:
        count = count + ok.astype(jnp.int32)

        @pl.when(ok)
        def _(to=to):
            pl.semaphore_signal(barrier, inc=1, device_id=to, device_id_type=pl.DeviceIdType.MESH)

    moves, stops, works, counts = schedule(n)
    for i in range(len(moves)):

        @pl.when(c * n + z == i)
        def _(i=i):
            for e, w in enumerate(moves[i]):
                table[e] = w
            for e, w in enumerate(stops[i]):
                ends[e] = w

    bits = [lax.rem(lax.div(c * n + z, 2**i), 2) == 1 for i in range(4)]
    steps = len(works[0])
    units = [pick([w[t] for w in works], bits) for t in range(steps)]
    active = pick(counts, bits)

    fetch.wait()
    seg = seg_here[...].astype(jnp.float32)
    docs = lax.broadcasted_iota(jnp.int32, (HEAD_DIM, tok), 0).astype(jnp.float32)
    before = jnp.where(seg < docs, 1.0, 0.0).astype(jnp.bfloat16)
    counted = lax.dot_general(
        jnp.ones((16, tok), jnp.bfloat16), before, (((1,), (1,)), ((), ())), preferred_element_type=jnp.float32
    ).astype(jnp.bfloat16)
    wide = jnp.broadcast_to(seg, (16, tok)).astype(jnp.bfloat16)
    c_in[...] = counted
    s_in[...] = wide
    segs[k] = wide
    for j in range(2):
        kv[here + j, k, 2 * tok : 2 * tok + 16, :] = counted
    m_ref[...] = jnp.full_like(m_ref, LOW)
    acc[...] = jnp.zeros_like(acc)
    pl.semaphore_wait(barrier, count)
    for copy in theirs:
        copy.start()

    def link(d, unit, b):
        return pltpu.make_async_remote_copy(
            src_ref=kv.at[unit, b], dst_ref=kv.at[unit, b],
            send_sem=link_send.at[d, unit, b], recv_sem=link_recv.at[unit, b],
            device_id=peers[d][1], device_id_type=pl.DeviceIdType.MESH,
        )

    def decode(e):
        w = table[e]
        op, w = lax.rem(w, 8), lax.div(w, 8)
        b, w = lax.rem(w, 2), lax.div(w, 2)
        mask, unit = lax.rem(w, 16), lax.div(w, 16)
        return op, lax.rem(b + k, 2), mask, unit

    def query_block(b):
        onehot = lax.broadcasted_iota(jnp.int32, (HEAD_DIM, tok), 0).astype(jnp.float32)
        onehot = (segs[b, 0:1, :].astype(jnp.float32) == onehot).astype(jnp.bfloat16)
        at = slice(b * tok, (b + 1) * tok)
        for h in range(heads):
            qt[h, 0:HEAD_DIM, at] = qraw[b, :, h * HEAD_DIM : (h + 1) * HEAD_DIM].T
            qt[h, HEAD_DIM:, at] = onehot

    def body(unit, masked):
        j = lax.rem(unit, 2)
        keys, values = [], []
        for b in range(2):
            counts = kv[unit, b, 2 * tok : 2 * tok + 1, :].astype(jnp.float32)
            at = lax.broadcasted_iota(jnp.int32, (tok, HEAD_DIM), 0).astype(jnp.float32)
            shut = jnp.where(at < counts, LOW, 0.0).astype(jnp.bfloat16)
            keys.append(jnp.concatenate([kv[unit, b, 0:tok, :], shut], axis=1))
            vt = kv[unit, b, tok : 2 * tok, :].T
            values.append(jnp.concatenate([vt, jnp.ones((16, tok), jnp.bfloat16)], axis=0))
        tiles = [(i, q) for i in range(group) for q in range(2)]

        def scores(i, q):
            right = qt[group * j + i, :, q * tok : (q + 1) * tok]
            return [jnp.dot(keys[b], right, preferred_element_type=jnp.float32) for b in range(2)]

        def summed(i, q, ps, alpha):
            pv = sum(jnp.dot(values[b], ps[b], preferred_element_type=jnp.float32) for b in range(2))
            at = slice(q * tok, (q + 1) * tok)
            acc[group * j + i, :, at] = acc[group * j + i, :, at] * alpha + pv

        AHEAD = 2
        ready = [scores(*u) for u in tiles[:AHEAD]]
        waiting = None
        for pos, (i, q) in enumerate(tiles):
            if pos + AHEAD < len(tiles):
                ready.append(scores(*tiles[pos + AHEAD]))
            ss = ready.pop(0)
            if masked is not None:
                sign, shift = masked
                diff = lax.broadcasted_iota(jnp.int32, (tok, tok), 0) - lax.broadcasted_iota(jnp.int32, (tok, tok), 1)
                ss = [jnp.where(sign * (diff + (b - q) * tok) + shift <= 0, ss[b], LOW) for b in range(2)]
            at = slice(q * tok, (q + 1) * tok)
            m_old = m_ref[group * j + i, :, at]
            m_new = m_old
            for x in ss:
                m_new = jnp.maximum(m_new, jnp.max(x, axis=0, keepdims=True))
            ps = [jnp.exp2((x - m_new) * scale).astype(jnp.bfloat16) for x in ss]
            alpha = jnp.exp2((m_old - m_new) * scale)
            m_ref[group * j + i, :, at] = m_new
            if waiting is not None:
                summed(*waiting)
            waiting = (i, q, ps, alpha)
        summed(*waiting)

    def entry(e, carry):
        op, b, mask, unit = decode(e)

        @pl.when(op == LOCAL)
        def _():
            for j in range(2):

                @pl.when(unit == here + j)
                def _(j=j):
                    for t in range(2):
                        mine[3 * j + t].wait()

        @pl.when(op == SIBLING)
        def _():
            for j in range(2):

                @pl.when(unit == here + j)
                def _(j=j):
                    for t in range(3):
                        coming(j, t).wait_recv()

        @pl.when(op == LINK)
        def _():
            link(0, unit, b).wait_recv()

        for d in range(4):

            @pl.when(lax.rem(lax.div(mask, 2**d), 2) == 1)
            def _(d=d):
                link(d, unit, b).start()

        return carry

    def step(t, carry):
        lax.fori_loop(jnp.where(t == 0, first, ends[jnp.maximum(t - 1, 0)]), ends[t], entry, 0)
        unit = pick(units, [lax.rem(lax.div(t, 2**i), 2) == 1 for i in range(steps.bit_length())])
        slab = lax.div(unit, 2)
        back, at = c - lax.div(slab, n), lax.rem(slab, n)
        rim = (at == z) & ((back == 0) | (back == 2))

        @pl.when((t < active) & rim)
        def _():
            sign = jnp.where(back == 0, 1, -1)
            body(unit, (sign, jnp.where(back == 0, 0, 1)))

        @pl.when((t < active) & jnp.logical_not(rim))
        def _():
            body(unit, None)

        return carry

    first = 4
    lax.fori_loop(0, first, entry, 0)
    mine[6].wait()
    for i in (6, 7):
        ref = (qraw, segs)[i - 6].at[1 - k]
        to_sib(ref, ref, i).wait_recv()
    for b in range(2):
        query_block(b)
    lax.fori_loop(0, steps, step, 0)
    lax.fori_loop(ends[steps - 1], ends[steps], entry, 0)

    for h in range(heads):
        total = acc[h, HEAD_DIM : HEAD_DIM + 1, :]
        out = acc[h, 0:HEAD_DIM, :] * (1.0 / total)
        logs = m_ref[h] * (1.0 / math.sqrt(HEAD_DIM)) + jnp.log(total)
        for b in range(2):
            at = slice(b * tok, (b + 1) * tok)
            obuf[b, :, h * HEAD_DIM : (h + 1) * HEAD_DIM] = out[:, at].T.astype(obuf.dtype)
            lsbuf[b, h : h + 1, :] = logs[:, at]
    cols = pl.ds(pl.multiple_of(k * heads * HEAD_DIM, HEAD_DIM), heads * HEAD_DIM)
    rows = pl.ds(pl.multiple_of(k * heads, heads), heads)
    back = [to_sib(obuf.at[1 - k], o_out.at[:, cols], 8), to_sib(lsbuf.at[1 - k], ls_out.at[rows, :], 9)]
    keep = [
        pltpu.make_async_copy(obuf.at[k], o_out.at[:, cols], local.at[8]),
        pltpu.make_async_copy(lsbuf.at[k], ls_out.at[rows, :], local.at[9]),
    ]
    for copy in back + keep:
        copy.start()

    def finish(e, carry):
        _, b, mask, unit = decode(e)
        for d in range(4):

            @pl.when(lax.rem(lax.div(mask, 2**d), 2) == 1)
            def _(d=d):
                link(d, unit, b).wait_send()

        return carry

    lax.fori_loop(0, ends[steps], finish, 0)
    for copy in theirs + back:
        copy.wait_send()
    other = pl.ds(pl.multiple_of((1 - k) * heads * HEAD_DIM, HEAD_DIM), heads * HEAD_DIM)
    low = pl.ds(pl.multiple_of((1 - k) * heads, heads), heads)
    to_sib(obuf.at[k], o_out.at[:, other], 8).wait_recv()
    to_sib(lsbuf.at[k], ls_out.at[low, :], 9).wait_recv()
    for copy in keep:
        copy.wait()


def fused(queries, key_rows, value_rows, segments):
    n = lax.axis_size("seq") // 2
    tok = queries.shape[0]
    heads = Q_HEADS // 2
    hbm = pl.BlockSpec(memory_space=pltpu.HBM)
    units = 8 * n
    moves, stops, _, _ = schedule(n)
    return pl.pallas_call(
        functools.partial(exchange_attend, n),
        out_shape=[
            jax.ShapeDtypeStruct(queries.shape, jnp.bfloat16),
            jax.ShapeDtypeStruct((Q_HEADS, tok), jnp.float32),
        ],
        in_specs=[hbm] * 4,
        out_specs=[pl.BlockSpec(memory_space=pl.ANY)] * 2,
        scratch_shapes=[
            pltpu.SMEM((max(len(m) for m in moves),), jnp.int32),
            pltpu.SMEM((len(stops[0]),), jnp.int32),
            pltpu.VMEM((16, HEAD_DIM), jnp.bfloat16),
            pltpu.VMEM((16, tok), jnp.bfloat16),
            pltpu.VMEM((units, 2, 2 * tok + 16, HEAD_DIM), jnp.bfloat16),
            pltpu.VMEM((2, tok, heads * HEAD_DIM), jnp.bfloat16),
            pltpu.VMEM((2, 16, tok), jnp.bfloat16),
            pltpu.VMEM((heads, 2 * HEAD_DIM, 2 * tok), jnp.bfloat16),
            pltpu.VMEM((heads, 1, 2 * tok), jnp.float32),
            pltpu.VMEM((heads, HEAD_DIM + 16, 2 * tok), jnp.float32),
            pltpu.VMEM((2, tok, heads * HEAD_DIM), jnp.bfloat16),
            pltpu.VMEM((2, heads, tok), jnp.float32),
            pltpu.VMEM((1, tok), jnp.int32),
            pltpu.SemaphoreType.DMA((10,)),
            pltpu.SemaphoreType.DMA((10,)),
            pltpu.SemaphoreType.DMA((10,)),
            pltpu.SemaphoreType.DMA((4, units, 2)),
            pltpu.SemaphoreType.DMA((units, 2)),
        ],
        compiler_params=pltpu.CompilerParams(
            collective_id=0, has_side_effects=True, vmem_limit_bytes=24 * 1024 * 1024
        ),
    )(*(pltpu.with_memory_space_constraint(x, pltpu.HBM) for x in (key_rows, value_rows, queries, segments[None, :])))


def on_device(queries, key_rows, value_rows, segments):
    tok = queries.shape[0]
    grp_n, seq_n = lax.axis_size("grp"), lax.axis_size("seq")
    device = lax.axis_index(AXES)
    offset = device * tok
    if grp_n == 4 and seq_n == 8 and 2 * seq_n * tok == WINDOW and tok <= 256:
        return fused(queries, key_rows, value_rows, segments)
    k_all = lax.all_gather(key_rows, AXES)
    v_all = lax.all_gather(value_rows, AXES)
    seg_all = lax.all_gather(segments, AXES)
    base = 0
    seg_all = seg_all.reshape(-1)
    key_pos = base * tok + jnp.arange(seg_all.shape[0], dtype=jnp.int32)
    begin = jnp.maximum(offset - WINDOW, 0)
    before = (key_pos >= begin) & (key_pos < offset) & (seg_all < segments[0])
    carried = begin + jnp.sum(before.astype(jnp.int32))
    inner = jnp.sum((segments[:, None] < segments[None, :]).astype(jnp.int32), axis=0)
    starts = jnp.where(segments == segments[0], carried, offset + inner)
    positions = offset + jnp.arange(tok, dtype=jnp.int32)
    lower = jnp.maximum(starts, positions - WINDOW + 1)
    first = jnp.min(lower) // tok
    clean = (jnp.max(lower) + tok - 1) // tok
    info = jnp.stack([device, first, clean, device - base]).astype(jnp.int32)
    reach = (WINDOW - 1 + tok - 1) // tok + 1
    return attention(info, lower, queries, k_all, v_all, reach)


def attention(info, lower, queries, k_all, v_all, reach):
    tok = queries.shape[0]
    width = k_all.shape[2]

    def kv_index(j, info):
        return (jnp.maximum(info[3] - j, info[3] - info[0] + info[1]), 0, 0)

    const = lambda j, info: (0, 0)
    return pl.pallas_call(
        flash,
        grid_spec=pltpu.PrefetchScalarGridSpec(
            num_scalar_prefetch=1,
            grid=(reach,),
            in_specs=[
                pl.BlockSpec((1, tok), const),
                pl.BlockSpec(queries.shape, const),
                pl.BlockSpec((None, tok, width), kv_index),
                pl.BlockSpec((None, tok, width), kv_index),
            ],
            out_specs=[
                pl.BlockSpec(queries.shape, const),
                pl.BlockSpec((Q_HEADS, tok), const),
            ],
            scratch_shapes=[
                pltpu.VMEM((Q_HEADS, HEAD_DIM, tok), jnp.bfloat16),
                pltpu.VMEM((Q_HEADS, 1, tok), jnp.float32),
                pltpu.VMEM((Q_HEADS, 1, tok), jnp.float32),
                pltpu.VMEM((Q_HEADS, HEAD_DIM, tok), jnp.float32),
                pltpu.VMEM((tok, tok), jnp.float32),
            ],
        ),
        out_shape=[
            jax.ShapeDtypeStruct(queries.shape, jnp.bfloat16),
            jax.ShapeDtypeStruct((Q_HEADS, tok), jnp.float32),
        ],
        compiler_params=pltpu.CompilerParams(dimension_semantics=("arbitrary",)),
    )(info, lower[None, :], queries, k_all, v_all)


def solution(mesh):
    in_specs = (P(AXES, None), P(AXES, None), P(AXES, None), P(AXES))
    out_specs = (P(AXES, None), P(None, AXES))
    return jax.shard_map(
        on_device, mesh=mesh, in_specs=in_specs, out_specs=out_specs, check_vma=False
    )
```

profile of v0, /device:TPU:5, one launch (start us, length us, event | category | flops | bytes accessed | tf_op | source)
XLA Modules:
  0.0 58.1 jit_solution(16878432002284766381)
XLA Ops:
  0.6 55.9 %shard_map.59 = (bf16[256,2048]{1,0:T(8,128)(2,1)S(1)}, f32[16,256]{1,0:T(8,128)S(1)}) custom-call(bf16[256,512]{1,0:T(8,128)(2,1)} %k_in.1, bf16[256,512]{1,0:T(8,128)(2,1)} %v_in.1, bf16[256,2048]{1,0:T(8,128)(2,1)} %q_in.1, s32[1,256]{1,0:T(1,128)} %bitcast.1), custom_call_target="tpu_custom_call" | custom-call | tf_op jit(solution)/shard_map/pallas_call | solution.py:522
  56.6 1.0 %copy.8 = bf16[256,2048]{1,0:T(8,128)(2,1)} copy(bf16[256,2048]{1,0:T(8,128)(2,1)S(1)} %get-tuple-element.4) | data formatting | bytes 2097152
  57.5 0.6 %copy.9 = f32[16,256]{1,0:T(8,128)} copy(f32[16,256]{1,0:T(8,128)S(1)} %get-tuple-element.5) | data formatting | bytes 32768
where the time goes:
time: 58.3 us; the launch traced here: 58.1 us
  Pallas kernels  55.9 us (96%)
  local copies, waits for them, and re-layouts  1.58 us (3%)
  between operations  0.64 us (1%)
    pallas_call x1, Pallas kernels, fused(): pl.pallas_call(functools.partial(exchange_attend, n), out_shape=[jax.Shap...  55.9 us
    unnamed x2, local copies, waits for them, and re-layouts  1.58 us

commit v1 on v0

--- a/solution.py
+++ b/solution.py
@@ -91,55 +91,21 @@
             ls_ref[h : h + 1, :] = m_ref[h] * (1.0 / math.sqrt(HEAD_DIM)) + jnp.log(l_ref[h])
 
 
-def routes(n, c, z, g, s, j):
-    other = z + 1 - 2 * (z % 2)
-    cross = not (s == other and j == 1)
-    near, far = s == 1 and j == 1, s == n - 1 and j == 1
-    up, down = z + 1 < n and s <= z, z > 0 and s >= z
-    out = []
-    if c in (0, 2) and g == c:
-        if up:
-            out.append(0)
-        if down and not (c == 2 and z == 1 and (near or far)):
-            out.append(1)
-        if cross and not (c == 2 and z == 0 and far):
-            out.append(2)
-        if c == 0 and s >= z and not (z == 0 and near):
-            out.append(3)
-    elif c == 0 and g == 1:
-        out.append(3)
-    elif c == 1 and g == 1:
-        if up:
-            out.append(0)
-        if down:
-            out.append(1)
-        if s < z and j == 1:
-            out.append(2)
-        elif not (z == 0 and near):
-            out.append(3)
-    elif c in (1, 3) and g == c - 1:
-        if s == z and j == 1:
-            out.append(z % 2)
-        elif c == 3 and z == 1 and far:
-            out.append(1)
-    elif c == 2:
-        if g == 0 and z == 1 and near:
-            out.append(1)
-        if g == 1 and (z in (1, n - 2) and far or z == 1 and s == n - 1):
-            out.append(1)
-    elif c == 3 and g == 3:
-        if up:
-            out.append(0)
-    elif c == 3 and g == 1:
-        if not (z <= 1 and far or z == 0 and s == n - 1):
-            out.append(2)
-        if z == 1 and near:
-            out.append(1)
-    return out
-
-
-def step_to(c, z, d):
-    return ((c, z + 1), (c, z - 1), (c ^ 1, z), (c ^ 2, z))[d]
+ROUTES = (
+    1855310, 1855310, 1758440, 1758565, 4890511576, 9650953, 8464676, 8488425, 42791646, 4929557131, 44727131,
+    44816506, 122230363153, 213566280, 213541355, 213542606, 125661521875, 123237693825, 4858872225, 1099025020,
+    4608094065, 18200594475, 3659955416, 125683000715, 29780628525, 29780628575, 18034925391, 24382191625,
+    133541425450, 144445703125, 151057046875, 130285546875, 114378906250, 114378906250, 82642578125, 108275390625,
+    83417968750, 113886718750, 100947656250, 107051171875, 111425781250, 111425781250, 99218750000, 111425781250,
+    113049218750, 114269921875, 99121093750, 99121093750, 75683593750, 75683593750, 75683593750, 75683593750,
+    73242187500, 73242187500, 73242187500, 73242187500, 61035156250, 61035156250, 61035156250, 61035156250, 0, 0, 0,
+    0,
+)
+EARLY = (
+    5, -3, -6.5, -2, 2.5, -5, 9.5, -2.5, -5, -7.5, 2, 9, -4, -6.5, 1, 4.5, -2, -2, 2, 1.5, -3, -0.5, 1, 10.5, 6,
+    -5.5, -5.5, 0, -8, -11, -7.5, 6.5, 0.5, 1.5, -4, -10, -3, 2.5, 7.5, 4, -6.5, -5, 1.5, 1.5, -2, -5, 8, 8, -3, 11,
+    -0.5, 12, 6.5, -3, 8.5, 0.5, 0, -3.5, 8, -6, 4, 9.5, 3.5, -1.5,
+)
 
 
 def needed(c, z, g, s):
@@ -149,87 +115,95 @@
 LOCAL, SIBLING, LINK, SEND, COMPUTE = range(5)
 
 
-def schedule(n, chunk=2.95, flight=1.7, work=1.8, ahead=2.5, ready=4.5):
+def schedule(n, chunk=2.95, flight=1.7, work=1.8, ahead=2.8, ready=5.0):
     chips = [(c, z) for c in range(4) for z in range(n)]
-
-    @functools.lru_cache(None)
-    def depth(c, z, g, s, j):
-        return max((1 + depth(*step_to(c, z, d), g, s, j) for d in routes(n, c, z, g, s, j)), default=0)
-
-    free, seen, inbox, pend, have, clock, prog, todo = {}, {}, {}, {}, {}, {}, {}, {}
-    order = 0
+    near = []
     for c, z in chips:
-        ch = c, z
-        own = [(2.0 + 1.5 * b, -j, (c, z, j, b)) for b in (0, 1) for j in (1, 0)]
-        inbox[ch], have[ch], clock[ch], prog[ch], todo[ch] = own, [], 2.0, [], []
-        seen[ch] = [u for _, _, u in own]
-        for d in range(4):
-            free[ch, d], pend[ch, d] = 0.0, []
-
-    def issue(ch, d, t):
-        u = heapq.heappop(pend[ch, d])[2]
-        to = step_to(*ch, d)
-        free[ch, d] = max(free[ch, d], t) + chunk
-        assert u not in seen[to]
-        seen[to].append(u)
-        heapq.heappush(inbox[to], (free[ch, d] + flight, 0, u))
-        return u
-
-    def options(ch):
-        t = clock[ch]
-        for d in range(4):
-            if pend[ch, d]:
-                yield max(t, free[ch, d] - ahead), 0, ch, d
-        if inbox[ch]:
-            yield max(t, inbox[ch][0][0]), 1, ch, 0
-        if todo[ch]:
-            yield max(t, ready), 2, ch, 0
-
-    while True:
-        best = min((o for ch in chips for o in options(ch)), default=None)
-        if best is None:
-            break
-        t, kind, ch, d = best
+        ways = ((c, z + 1), (c, z - 1), (c ^ 1, z), (c ^ 2, z))
+        near.append([chips.index(w) if w in chips else None for w in ways])
+    count = len(chips)
+    home = [chip for chip in range(count) for _ in range(4)]
+    kids, depth = [], []
+    for code in ROUTES:
+        above = []
+        for chip in range(count):
+            code, way = divmod(code, 5)
+            above.append(near[chip][way - 1] if way else None)
+        kid, deep = [[] for _ in chips], [0] * count
+        for chip in range(count):
+            if above[chip] is not None:
+                kid[above[chip]].append(near[above[chip]].index(chip))
+                far, hops = chip, 0
+                while above[far] is not None:
+                    far, hops = above[far], hops + 1
+                    deep[far] = max(deep[far], hops)
+        kids.append(kid)
+        depth.append(deep)
+
+    free = [[0.0] * 4 for _ in chips]
+    pend = [[[] for _ in range(4)] for _ in chips]
+    inbox = [sorted((2.0 + 1.5 * b, -j, i * 4 + j * 2 + b) for b in (0, 1) for j in (1, 0)) for i in range(count)]
+    have, todo, prog = [[] for _ in chips], [[] for _ in chips], [[] for _ in chips]
+    clock, order = [2.0] * count, 0
+
+    def option(i):
+        found = [(max(free[i][d] - ahead, clock[i]), 0, d) for d in range(4) if pend[i][d]]
+        if inbox[i]:
+            found.append((max(inbox[i][0][0], clock[i]), 1, 0))
+        if todo[i]:
+            found.append((max(clock[i], ready), 2, 0))
+        return min(found, default=None)
+
+    def issue(i, d, t):
+        q = heapq.heappop(pend[i][d])[2]
+        to = near[i][d]
+        free[i][d] = max(free[i][d], t) + chunk
+        heapq.heappush(inbox[to], (free[i][d] + flight, 0, q))
+        choice[to] = option(to)
+        return q
+
+    choice = [option(i) for i in range(count)]
+    while any(o is not None for o in choice):
+        t, i = min((o[0], i) for i, o in enumerate(choice) if o is not None)
+        _, kind, d = choice[i]
         if kind == 0:
-            prog[ch].append((SEND, issue(ch, d, t), 1 << d))
-            clock[ch] = t + 0.05
+            prog[i].append((SEND, issue(i, d, t), 1 << d))
+            clock[i] = t + 0.07
         elif kind == 1:
-            u = heapq.heappop(inbox[ch])[2]
-            g, s, j, b = u
+            q = heapq.heappop(inbox[i])[2]
             mask = 0
-            for d in routes(n, *ch, g, s, j):
+            for d in kids[q][i]:
                 order += 1
-                heapq.heappush(pend[ch, d], (-depth(*step_to(*ch, d), g, s, j), order, u))
-                if free[ch, d] - ahead <= t and pend[ch, d][0][2] == u:
-                    issue(ch, d, t)
+                heapq.heappush(pend[i][d], (-depth[q][near[i][d]] - EARLY[q], order, q))
+                if free[i][d] - ahead <= t and pend[i][d][0][2] == q:
+                    issue(i, d, t)
                     mask |= 1 << d
-            op = LINK if (g, s) != ch else (LOCAL, SIBLING)[b]
-            prog[ch].append((op, u, mask))
-            clock[ch] = t + 0.1
-            have[ch].append(u)
-            if needed(*ch, g, s) and (g, s, j, 1 - b) in have[ch]:
-                todo[ch].append((g, s, j, 0))
+            prog[i].append((LINK if home[q] != i else (LOCAL, SIBLING)[q % 2], q, mask))
+            clock[i] = t + 0.12
+            have[i].append(q)
+            if needed(*chips[i], *chips[home[q]]) and q ^ 1 in have[i]:
+                todo[i].append(q // 2)
         else:
-            todo[ch].sort(key=lambda u: (u[0], u[1]) != ch)
-            prog[ch].append((COMPUTE, todo[ch].pop(0), 0))
-            clock[ch] = max(t, ready) + work
-    for ch in chips:
-        done = [u[:3] for op, u, _ in prog[ch] if op == COMPUTE]
-        want = [(g, s, j) for g in range(4) for s in range(n) for j in range(2) if needed(*ch, g, s)]
-        assert sorted(done) == want
-
-    def word(op, u, mask):
-        g, s, j, b = u
-        return op + 8 * (b + 2 * (mask + 16 * ((g * n + s) * 2 + j)))
+            todo[i].sort(key=lambda u: u // 2 != i)
+            prog[i].append((COMPUTE, todo[i].pop(0) * 2, 0))
+            clock[i] = t + work
+        choice[i] = option(i)
+    for i in range(count):
+        assert len(have[i]) == len(set(have[i]))
+        done = sorted(q // 2 for op, q, _ in prog[i] if op == COMPUTE)
+        assert done == [u for u in range(2 * count) if needed(*chips[i], *chips[u // 2])]
+
+    def word(op, q, mask):
+        return op + 8 * (q % 2 + 2 * (mask + 16 * (q // 2)))
 
     moves, stops, works = [], [], []
-    for ch in chips:
+    for entries in prog:
         stop, work = [], []
-        for op, u, _ in prog[ch]:
+        for place, (op, q, _) in enumerate(entries):
             if op == COMPUTE:
-                stop.append(len([e for e in prog[ch][: prog[ch].index((op, u, 0))] if e[0] != COMPUTE]))
-                work.append((u[0] * n + u[1]) * 2 + u[2])
-        move = [word(*e) for e in prog[ch] if e[0] != COMPUTE]
+                stop.append(place - len(work))
+                work.append(q // 2)
+        move = [word(*e) for e in entries if e[0] != COMPUTE]
         moves.append(move)
         stops.append(stop + [len(move)])
         works.append(work)
@@ -237,7 +211,10 @@
     counts = [len(w) for w in works]
     stops = [s[:-1] + [s[-1]] * (steps + 1 - len(s) + 1) for s in stops]
     works = [w + [w[-1]] * (steps - len(w)) for w in works]
-    return moves, stops, works, counts
+    sends = [
+        [d + 4 * (w // 8 % 2 + 2 * (w // 256)) for w in move for d in range(4) if w // 16 // 2**d % 2] for move in moves
+    ]
+    return moves, stops, works, counts, sends
 
 
 def pick(words, bits):
@@ -252,7 +229,7 @@
     return words[0]
 
 
-def exchange_attend(n, k_in, v_in, q_in, seg_in, o_out, ls_out, table, ends, c_in, s_in, kv, qraw, segs, qt, m_ref, acc, obuf, lsbuf, seg_here,
+def exchange_attend(n, k_in, v_in, q_in, seg_in, o_out, ls_out, table, ends, sent, c_in, s_in, kv, qraw, segs, qt, m_ref, acc, obuf, lsbuf, seg_here,
                     local, sib_send, sib_recv, link_send, link_recv):
     tok = k_in.shape[0]
     heads = Q_HEADS // 2
@@ -310,15 +287,17 @@
         def _(to=to):
             pl.semaphore_signal(barrier, inc=1, device_id=to, device_id_type=pl.DeviceIdType.MESH)
 
-    moves, stops, works, counts = schedule(n)
+    moves, stops, works, counts, sends = schedule(n)
     for i in range(len(moves)):
 
         @pl.when(c * n + z == i)
         def _(i=i):
             for e, w in enumerate(moves[i]):
                 table[e] = w
-            for e, w in enumerate(stops[i]):
+            for e, w in enumerate(stops[i] + [len(sends[i])]):
                 ends[e] = w
+            for e, w in enumerate(sends[i]):
+                sent[e] = w
 
     bits = [lax.rem(lax.div(c * n + z, 2**i), 2) == 1 for i in range(4)]
     steps = len(works[0])
@@ -338,8 +317,6 @@
     segs[k] = wide
     for j in range(2):
         kv[here + j, k, 2 * tok : 2 * tok + 16, :] = counted
-    m_ref[...] = jnp.full_like(m_ref, LOW)
-    acc[...] = jnp.zeros_like(acc)
     pl.semaphore_wait(barrier, count)
     for copy in theirs:
         copy.start()
@@ -361,7 +338,7 @@
     def query_block(b):
         onehot = lax.broadcasted_iota(jnp.int32, (HEAD_DIM, tok), 0).astype(jnp.float32)
         onehot = (segs[b, 0:1, :].astype(jnp.float32) == onehot).astype(jnp.bfloat16)
-        at = slice(b * tok, (b + 1) * tok)
+        at = pl.ds(pl.multiple_of(b * tok, HEAD_DIM), tok)
         for h in range(heads):
             qt[h, 0:HEAD_DIM, at] = qraw[b, :, h * HEAD_DIM : (h + 1) * HEAD_DIM].T
             qt[h, HEAD_DIM:, at] = onehot
@@ -463,52 +440,76 @@
         return carry
 
     first = 4
-    lax.fori_loop(0, first, entry, 0)
+    lax.fori_loop(0, 2, entry, 0)
+    m_ref[...] = jnp.full_like(m_ref, LOW)
+    acc[...] = jnp.zeros_like(acc)
     mine[6].wait()
+    query_block(k)
+    lax.fori_loop(2, first, entry, 0)
     for i in (6, 7):
         ref = (qraw, segs)[i - 6].at[1 - k]
         to_sib(ref, ref, i).wait_recv()
-    for b in range(2):
-        query_block(b)
+    query_block(1 - k)
     lax.fori_loop(0, steps, step, 0)
     lax.fori_loop(ends[steps - 1], ends[steps], entry, 0)
 
-    for h in range(heads):
-        total = acc[h, HEAD_DIM : HEAD_DIM + 1, :]
-        out = acc[h, 0:HEAD_DIM, :] * (1.0 / total)
-        logs = m_ref[h] * (1.0 / math.sqrt(HEAD_DIM)) + jnp.log(total)
-        for b in range(2):
-            at = slice(b * tok, (b + 1) * tok)
-            obuf[b, :, h * HEAD_DIM : (h + 1) * HEAD_DIM] = out[:, at].T.astype(obuf.dtype)
-            lsbuf[b, h : h + 1, :] = logs[:, at]
-    cols = pl.ds(pl.multiple_of(k * heads * HEAD_DIM, HEAD_DIM), heads * HEAD_DIM)
     rows = pl.ds(pl.multiple_of(k * heads, heads), heads)
-    back = [to_sib(obuf.at[1 - k], o_out.at[:, cols], 8), to_sib(lsbuf.at[1 - k], ls_out.at[rows, :], 9)]
-    keep = [
-        pltpu.make_async_copy(obuf.at[k], o_out.at[:, cols], local.at[8]),
-        pltpu.make_async_copy(lsbuf.at[k], ls_out.at[rows, :], local.at[9]),
-    ]
-    for copy in back + keep:
-        copy.start()
+    low = pl.ds(pl.multiple_of((1 - k) * heads, heads), heads)
+
+    def strip(core, j):
+        width = group * HEAD_DIM
+        return pl.ds(pl.multiple_of((2 * core + j) * width, width), width)
+
+    back, keep = [], []
+    for j in range(2):
+        for h in range(group * j, group * (j + 1)):
+            total = acc[h, HEAD_DIM : HEAD_DIM + 1, :]
+            out = acc[h, 0:HEAD_DIM, :] * (1.0 / total)
+            logs = m_ref[h] * (1.0 / math.sqrt(HEAD_DIM)) + jnp.log(total)
+            for b in range(2):
+                at = slice(b * tok, (b + 1) * tok)
+                at_h = slice((h - group * j) * HEAD_DIM, (h - group * j + 1) * HEAD_DIM)
+                obuf[j, b, :, at_h] = out[:, at].astype(obuf.dtype).T
+                lsbuf[b, h : h + 1, :] = logs[:, at]
+        back.append(to_sib(obuf.at[j, 1 - k], o_out.at[:, strip(k, j)], (8, 10)[j]))
+        keep.append(pltpu.make_async_copy(obuf.at[j, k], o_out.at[:, strip(k, j)], local.at[(8, 10)[j]]))
+        back[j].start()
+        keep[j].start()
+    back.append(to_sib(lsbuf.at[1 - k], ls_out.at[rows, :], 9))
+    keep.append(pltpu.make_async_copy(lsbuf.at[k], ls_out.at[rows, :], local.at[9]))
+    back[2].start()
+    keep[2].start()
 
     def finish(e, carry):
-        _, b, mask, unit = decode(e)
-        for d in range(4):
-
-            @pl.when(lax.rem(lax.div(mask, 2**d), 2) == 1)
-            def _(d=d):
-                link(d, unit, b).wait_send()
-
+        w = sent[e]
+        d, w = lax.rem(w, 4), lax.div(w, 4)
+        ref = kv.at[lax.div(w, 2), lax.rem(lax.rem(w, 2) + k, 2)]
+        pltpu.make_async_remote_copy(
+            src_ref=ref, dst_ref=ref,
+            send_sem=link_send.at[d, lax.div(w, 2), lax.rem(lax.rem(w, 2) + k, 2)], recv_sem=sib_recv.at[0],
+            device_id=(c, sib), device_id_type=pl.DeviceIdType.MESH,
+        ).wait_send()
         return carry
 
-    lax.fori_loop(0, ends[steps], finish, 0)
+    lax.fori_loop(0, ends[steps + 1], finish, 0)
     for copy in theirs + back:
         copy.wait_send()
-    other = pl.ds(pl.multiple_of((1 - k) * heads * HEAD_DIM, HEAD_DIM), heads * HEAD_DIM)
-    low = pl.ds(pl.multiple_of((1 - k) * heads, heads), heads)
-    to_sib(obuf.at[k], o_out.at[:, other], 8).wait_recv()
+    for j in range(2):
+        to_sib(obuf.at[j, k], o_out.at[:, strip(1 - k, j)], (8, 10)[j]).wait_recv()
     to_sib(lsbuf.at[k], ls_out.at[low, :], 9).wait_recv()
     for copy in keep:
+        copy.wait()
+
+
+def store(o_in, ls_in, o_out, ls_out, sems):
+    copies = [pltpu.make_async_copy(ls_in, ls_out, sems.at[4])]
+    rows = o_in.shape[0] // 4
+    for i in range(4):
+        at = pl.ds(i * rows, rows)
+        copies.append(pltpu.make_async_copy(o_in.at[at, :], o_out.at[at, :], sems.at[i]))
+    for copy in copies:
+        copy.start()
+    for copy in copies:
         copy.wait()
 
 
@@ -518,18 +519,20 @@
     heads = Q_HEADS // 2
     hbm = pl.BlockSpec(memory_space=pltpu.HBM)
     units = 8 * n
-    moves, stops, _, _ = schedule(n)
-    return pl.pallas_call(
+    moves, stops, _, _, sends = schedule(n)
+    shapes = [
+        jax.ShapeDtypeStruct(queries.shape, jnp.bfloat16),
+        jax.ShapeDtypeStruct((Q_HEADS, tok), jnp.float32),
+    ]
+    held = pl.pallas_call(
         functools.partial(exchange_attend, n),
-        out_shape=[
-            jax.ShapeDtypeStruct(queries.shape, jnp.bfloat16),
-            jax.ShapeDtypeStruct((Q_HEADS, tok), jnp.float32),
-        ],
+        out_shape=shapes,
         in_specs=[hbm] * 4,
         out_specs=[pl.BlockSpec(memory_space=pl.ANY)] * 2,
         scratch_shapes=[
             pltpu.SMEM((max(len(m) for m in moves),), jnp.int32),
-            pltpu.SMEM((len(stops[0]),), jnp.int32),
+            pltpu.SMEM((len(stops[0]) + 1,), jnp.int32),
+            pltpu.SMEM((max(len(m) for m in sends),), jnp.int32),
             pltpu.VMEM((16, HEAD_DIM), jnp.bfloat16),
             pltpu.VMEM((16, tok), jnp.bfloat16),
             pltpu.VMEM((units, 2, 2 * tok + 16, HEAD_DIM), jnp.bfloat16),
@@ -538,12 +541,12 @@
             pltpu.VMEM((heads, 2 * HEAD_DIM, 2 * tok), jnp.bfloat16),
             pltpu.VMEM((heads, 1, 2 * tok), jnp.float32),
             pltpu.VMEM((heads, HEAD_DIM + 16, 2 * tok), jnp.float32),
-            pltpu.VMEM((2, tok, heads * HEAD_DIM), jnp.bfloat16),
+            pltpu.VMEM((2, 2, tok, heads // 2 * HEAD_DIM), jnp.bfloat16),
             pltpu.VMEM((2, heads, tok), jnp.float32),
             pltpu.VMEM((1, tok), jnp.int32),
-            pltpu.SemaphoreType.DMA((10,)),
-            pltpu.SemaphoreType.DMA((10,)),
-            pltpu.SemaphoreType.DMA((10,)),
+            pltpu.SemaphoreType.DMA((11,)),
+            pltpu.SemaphoreType.DMA((11,)),
+            pltpu.SemaphoreType.DMA((11,)),
             pltpu.SemaphoreType.DMA((4, units, 2)),
             pltpu.SemaphoreType.DMA((units, 2)),
         ],
@@ -551,6 +554,15 @@
             collective_id=0, has_side_effects=True, vmem_limit_bytes=24 * 1024 * 1024
         ),
     )(*(pltpu.with_memory_space_constraint(x, pltpu.HBM) for x in (key_rows, value_rows, queries, segments[None, :])))
+    anywhere = pl.BlockSpec(memory_space=pl.ANY)
+    return pl.pallas_call(
+        store,
+        out_shape=shapes,
+        in_specs=[anywhere] * 2,
+        out_specs=[anywhere] * 2,
+        scratch_shapes=[pltpu.SemaphoreType.DMA((5,))],
+        compiler_params=pltpu.CompilerParams(vmem_limit_bytes=1024 * 1024),
+    )(*held)
 
 
 def on_device(queries, key_rows, value_rows, segments):

time: 58.3 us -> 54.4 us (0.933)
  Pallas kernels: 55.9 us -> 53.6 us
  local copies, waits for them, and re-layouts: 1.58 us -> 0 us
    pallas_call x1 -> x2, Pallas kernels: 55.9 us -> 53.6 us  [the longest x1 52.6 us: fused(): pl.pallas_call(functools.partial(exchange_attend, n), out_shape=shapes, i...]
    unnamed x2 -> x0, local copies, waits for them, and re-layouts: 1.58 us -> none
where the time goes in v1:
time: 54.4 us; the launch traced here: 54.3 us
  Pallas kernels  53.6 us (99%)
  between operations  0.64 us (1%)
    pallas_call x1, Pallas kernels, fused(): pl.pallas_call(functools.partial(exchange_attend, n), out_shape=shapes, i...  52.6 us

profile of v1, /device:TPU:5, one launch (start us, length us, event | category | flops | bytes accessed | tf_op | source)
XLA Modules:
  0.0 54.3 jit_solution(1358340625534498257)
XLA Ops:
  0.6 52.6 %shard_map.59 = (bf16[256,2048]{1,0:T(8,128)(2,1)S(1)}, f32[16,256]{1,0:T(8,128)S(1)}) custom-call(bf16[256,512]{1,0:T(8,128)(2,1)} %k_in.1, bf16[256,512]{1,0:T(8,128)(2,1)} %v_in.1, bf16[256,2048]{1,0:T(8,128)(2,1)} %q_in.1, s32[1,256]{1,0:T(1,128)} %bitcast.1), custom_call_target="tpu_custom_call" | custom-call | tf_op jit(solution)/shard_map/pallas_call | solution.py:527
  53.2 1.0 %shard_map.60 = (bf16[256,2048]{1,0:T(8,128)(2,1)}, f32[16,256]{1,0:T(8,128)}) custom-call(bf16[256,2048]{1,0:T(8,128)(2,1)S(1)} %get-tuple-element.4.o_in, f32[16,256]{1,0:T(8,128)S(1)} %get-tuple-element.5.ls_in), custom_call_target="tpu_custom_call" | custom-call | tf_op jit(solution)/shard_map/pallas_call | solution.py:558

commit v2 on v1

--- a/solution.py
+++ b/solution.py
@@ -92,19 +92,19 @@
 
 
 ROUTES = (
-    1855310, 1855310, 1758440, 1758565, 4890511576, 9650953, 8464676, 8488425, 42791646, 4929557131, 44727131,
-    44816506, 122230363153, 213566280, 213541355, 213542606, 125661521875, 123237693825, 4858872225, 1099025020,
+    1839685, 1855310, 1758440, 1758565, 4890511576, 9650953, 8464676, 8488425, 42791646, 4929557131, 44727131,
+    44816506, 122230363153, 223331905, 213541355, 213542606, 125661521875, 123237693825, 4858872225, 1099025020,
     4608094065, 18200594475, 3659955416, 125683000715, 29780628525, 29780628575, 18034925391, 24382191625,
-    133541425450, 144445703125, 151057046875, 130285546875, 114378906250, 114378906250, 82642578125, 108275390625,
+    133541425450, 144445703125, 151057046875, 142492578125, 114378906250, 114378906250, 82642578125, 108275390625,
     83417968750, 113886718750, 100947656250, 107051171875, 111425781250, 111425781250, 99218750000, 111425781250,
     113049218750, 114269921875, 99121093750, 99121093750, 75683593750, 75683593750, 75683593750, 75683593750,
     73242187500, 73242187500, 73242187500, 73242187500, 61035156250, 61035156250, 61035156250, 61035156250, 0, 0, 0,
     0,
 )
 EARLY = (
-    5, -3, -6.5, -2, 2.5, -5, 9.5, -2.5, -5, -7.5, 2, 9, -4, -6.5, 1, 4.5, -2, -2, 2, 1.5, -3, -0.5, 1, 10.5, 6,
-    -5.5, -5.5, 0, -8, -11, -7.5, 6.5, 0.5, 1.5, -4, -10, -3, 2.5, 7.5, 4, -6.5, -5, 1.5, 1.5, -2, -5, 8, 8, -3, 11,
-    -0.5, 12, 6.5, -3, 8.5, 0.5, 0, -3.5, 8, -6, 4, 9.5, 3.5, -1.5,
+    5, -3, -6.5, -2, 2.5, -5, 9.5, -2.5, -5, -7.5, 2, 9, -4, -6.5, 1, 4.5, -2, -2, 2, 1.5, -3, 0, 1, 10.5, 6, -5.5,
+    -6, 0, -8, -11, -7.5, 6.5, 0.5, 1.5, -4, -10, -3, 2.5, 7.5, 4, -6.5, -5, 1.5, 1.5, -2, -5, 8, 8, -3, 11, -0.5,
+    12, 6.5, -3, 8.5, 0.5, 0, -3.5, 8, -6, 4, 9.5, 3.5, -1.5,
 )
 
 
@@ -353,7 +353,7 @@
             keys.append(jnp.concatenate([kv[unit, b, 0:tok, :], shut], axis=1))
             vt = kv[unit, b, tok : 2 * tok, :].T
             values.append(jnp.concatenate([vt, jnp.ones((16, tok), jnp.bfloat16)], axis=0))
-        tiles = [(i, q) for i in range(group) for q in range(2)]
+        tiles = [(i, q) for q in range(2) for i in range(group)]
 
         def scores(i, q):
             right = qt[group * j + i, :, q * tok : (q + 1) * tok]

time: 54.4 us -> 54.4 us (level)
  no operation moved by 1% of the time
where the time goes in v2:
time: 54.4 us; the launch traced here: 54.2 us
  Pallas kernels  53.6 us (99%)
  between operations  0.64 us (1%)
    pallas_call x1, Pallas kernels, fused(): pl.pallas_call(functools.partial(exchange_attend, n), out_shape=shapes, i...  52.6 us

profile of v2, /device:TPU:5, one launch (start us, length us, event | category | flops | bytes accessed | tf_op | source)
XLA Modules:
  0.0 54.2 jit_solution(16801330567469425594)
XLA Ops:
  0.6 52.6 %shard_map.59 = (bf16[256,2048]{1,0:T(8,128)(2,1)S(1)}, f32[16,256]{1,0:T(8,128)S(1)}) custom-call(bf16[256,512]{1,0:T(8,128)(2,1)} %k_in.1, bf16[256,512]{1,0:T(8,128)(2,1)} %v_in.1, bf16[256,2048]{1,0:T(8,128)(2,1)} %q_in.1, s32[1,256]{1,0:T(1,128)} %bitcast.1), custom_call_target="tpu_custom_call" | custom-call | tf_op jit(solution)/shard_map/pallas_call | solution.py:527
  53.2 1.0 %shard_map.60 = (bf16[256,2048]{1,0:T(8,128)(2,1)}, f32[16,256]{1,0:T(8,128)}) custom-call(bf16[256,2048]{1,0:T(8,128)(2,1)S(1)} %get-tuple-element.4.o_in, f32[16,256]{1,0:T(8,128)S(1)} %get-tuple-element.5.ls_in), custom_call_target="tpu_custom_call" | custom-call | tf_op jit(solution)/shard_map/pallas_call | solution.py:558
